TPU v7x, 32 devices: a whole 2x2x4 slice. The times are simulated.
32 devices in a mesh: dp: 4 (over y, x), tensor: 8 (over z, core).
Axes of the slice: x: 2, y: 2, z: 4, core: 2. Of those that a mesh axis runs over, the one named last changes fastest.
Arguments:
- tokens: bfloat16 [768, 4096], P(('dp', 'tensor')), may hold values from -6 to 6
- out_grad: bfloat16 [768, 4096], P(('dp', 'tensor')), may hold values from -6 to 6
- w_gate: bfloat16 [4096, 14336], P(None, 'tensor'), may hold values from -0.09375 to 0.09375
- w_up: bfloat16 [4096, 14336], P(None, 'tensor'), may hold values from -0.09375 to 0.09375
- w_down: bfloat16 [14336, 4096], P('tensor'), may hold values from -0.046875 to 0.046875
Outputs:
- grad_tokens: bfloat16 [768, 4096], P(('dp', 'tensor'))
- grad_gate: bfloat16 [4096, 14336], P('dp', 'tensor')
- grad_up: bfloat16 [4096, 14336], P('dp', 'tensor')
- grad_down: bfloat16 [14336, 4096], P('tensor', 'dp')
All inputs are finite; a program needn't handle non-finite values.
Results may differ from a plain program's by a relative error of at most 0.014.
Values may be sent and summed in bfloat16 or wider, within the bound.
No kernel may reach another device: no remote copies, remote signals or barrier semaphores. Data moves between devices by JAX's collectives and lax.ppermute only.
A program may use at most 128 MiB of HBM per device.

v0:
```python
import jax
import jax.numpy as jnp
from jax import lax
from jax.sharding import PartitionSpec as P


def contract_last(left, right):
    return lax.dot_general(
        left, right, (((1,), (1,)), ((), ())), preferred_element_type=jnp.float32
    )


def group_total(partials):
    rounded = partials.astype(jnp.bfloat16)
    rounded = lax.optimization_barrier(rounded)
    return jnp.sum(rounded.astype(jnp.float32), axis=0)


def per_device(tokens, out_grad, w_gate, w_up, w_down):
    group_tokens, group_grads = (
        lax.all_gather(tokens, "tensor", axis=0, tiled=True),
        lax.all_gather(out_grad, "tensor", axis=0, tiled=True),
    )
    gate_val = jnp.dot(group_tokens, w_gate, preferred_element_type=jnp.float32)
    up_val = jnp.dot(group_tokens, w_up, preferred_element_type=jnp.float32)
    sigmoid_gate = jax.nn.sigmoid(gate_val)
    act_val = gate_val * sigmoid_gate
    hidden = (act_val * up_val).astype(jnp.bfloat16)
    grad_hidden = contract_last(group_grads, w_down)
    grad_gate_pre = (
        grad_hidden * up_val * sigmoid_gate * (1.0 + gate_val * (1.0 - sigmoid_gate))
    ).astype(jnp.bfloat16)
    grad_up_pre = (grad_hidden * act_val).astype(jnp.bfloat16)
    grad_tokens = lax.psum_scatter(
        (contract_last(grad_gate_pre, w_gate) + contract_last(grad_up_pre, w_up)).astype(
            jnp.bfloat16
        ),
        "tensor",
        scatter_dimension=0,
        tiled=True,
    )
    groups = lax.axis_size("dp")
    group_rows = group_tokens.shape[0]
    tok_cols, grad_cols = (
        lax.all_to_all(group_tokens, "dp", split_axis=1, concat_axis=0, tiled=True),
        lax.all_to_all(group_grads, "dp", split_axis=1, concat_axis=0, tiled=True),
    )
    hid_all, gate_all, up_all = (
        lax.all_gather(hidden, "dp", axis=0, tiled=True),
        lax.all_gather(grad_gate_pre, "dp", axis=0, tiled=True),
        lax.all_gather(grad_up_pre, "dp", axis=0, tiled=True),
    )
    tok_split = tok_cols.reshape(groups, group_rows, -1)
    grad_split = grad_cols.reshape(groups, group_rows, -1)
    hid_split = hid_all.reshape(groups, group_rows, -1)
    gate_split = gate_all.reshape(groups, group_rows, -1)
    up_split = up_all.reshape(groups, group_rows, -1)
    sum_gate = group_total(
        jnp.einsum("gtd,gth->gdh", tok_split, gate_split, preferred_element_type=jnp.float32)
    )
    sum_up = group_total(
        jnp.einsum("gtd,gth->gdh", tok_split, up_split, preferred_element_type=jnp.float32)
    )
    sum_down = group_total(
        jnp.einsum("gth,gtd->ghd", hid_split, grad_split, preferred_element_type=jnp.float32)
    )
    return (
        grad_tokens,
        sum_gate.astype(jnp.bfloat16),
        sum_up.astype(jnp.bfloat16),
        sum_down.astype(jnp.bfloat16),
    )


def solution(mesh):
    in_specs = (
        P(("dp", "tensor"), None),
        P(("dp", "tensor"), None),
        P(None, "tensor"),
        P(None, "tensor"),
        P("tensor", None),
    )
    out_specs = (P(("dp", "tensor"), None), P("dp", "tensor"), P("dp", "tensor"), P("tensor", "dp"))
    return jax.shard_map(
        per_device, mesh=mesh, in_specs=in_specs, out_specs=out_specs, check_vma=False
    )
```

profile of v0, /device:TPU:0, one launch (start us, length us, event | category | flops | bytes accessed | tf_op | source)
XLA Modules:
  0.0 276.6 jit_solution(235035646883662496)
XLA Ops:
  7.2 0.0 all-gather.6.cloned.1.call-start
  7.2 0.7 all-gather.6.cloned.1.call-update
  7.9 0.0 all-gather.8.cloned.1.call-start
  7.9 0.7 all-gather.8.cloned.1.call-update
  8.6 0.0 all-gather.14.cloned.1.call-start
  8.7 28.9 %all-gather.6.cloned.1.call-done = bf16[192,4096]{1,0:T(8,128)(2,1)} async-done(((bf16[24,4096]{1,0:T(8,128)(2,1)}), bf16[192,4096]{1,0:T(8,128)(2,1)}) %all-gather.6.cloned.1.call-update) | async-done | bytes 1572880 | tf_op jit(solution)/shard_map/all_gather | solution.py:22
  37.6 8.6 %fusion.5 = f32[192,1792]{1,0:T(8,128)S(1)} fusion(bf16[192,4096]{1,0:T(8,128)(2,1)} %all-gather.6.cloned.1.call-done, bf16[1792,4096]{1,0:T(8,128)(2,1)} %param.9), kind=kOutput, calls=%fused_computation.15 | convolution fusion | flops 2818572288 | bytes 17629184 | tf_op jit(solution)/shard_map/dot_general | solution.py:8
  46.3 17.4 %all-gather.8.cloned.1.call-done = bf16[192,4096]{1,0:T(8,128)(2,1)} async-done(((bf16[24,4096]{1,0:T(8,128)(2,1)}), bf16[192,4096]{1,0:T(8,128)(2,1)}) %all-gather.8.cloned.1.call-update) | async-done | bytes 1572880 | tf_op jit(solution)/shard_map/all_gather | solution.py:21
  63.7 0.0 copy-start.1
  63.7 0.0 copy-start.4
  63.7 9.3 %fusion.6 = f32[192,1792]{1,0:T(8,128)S(1)} fusion(bf16[192,4096]{1,0:T(8,128)(2,1)} %all-gather.8.cloned.1.call-done, bf16[4096,1792]{1,0:T(8,128)(2,1)} %param.7), kind=kOutput, calls=%fused_computation.16 | convolution fusion | flops 2818572288 | bytes 17629184 | tf_op jit(solution)/shard_map/dot_general | solution.py:24
  73.0 0.0 copy-done.1
  73.0 1.0 copy-done.4
  74.0 4.8 %multiply_convert_fusion = (bf16[192,1792]{1,0:T(8,128)(2,1)}, bf16[192,1792]{1,0:T(8,128)(2,1)}, bf16[192,1792]{1,0:T(8,128)(2,1)}) fusion(f32[192,1792]{1,0:T(8,128)S(1)} %fusion.6, f32[192,1792]{1,0:T(8,128)S(1)} %fusion.5, bf16[192,4096]{1,0:T(8,128)(2,1)S(1)} %copy-done.1, bf16[4096,1792]{1,0:T(8,128)(2,1)S(1)} %copy-done.4), kind=kOutput, calls=%fused_computation.10 | convolution fusion | flops 2823733248 | bytes 21069824 | tf_op jit(solution)/shard_map/dot_general | solution.py:25
  78.7 0.0 copy-start
  78.7 0.0 all-gather.14.cloned.1.call-update
  78.8 0.0 all-gather.12.cloned.1.call-start
  78.8 0.5 all-gather.12.cloned.1.call-update
  79.4 0.0 all-gather.10.cloned.1.call-start
  79.4 0.5 all-gather.10.cloned.1.call-update
  79.9 0.2 copy-done
  80.2 1.3 copy.19
  81.5 0.0 copy-start.2
  81.5 3.8 %all-to-all-start.1 = ((bf16[192,4,1024]{2,0,1:T(8,128)(2,1)}), bf16[192,4,1024]{2,0,1:T(8,128)(2,1)S(1)}, u32[]{:S(2)}, u32[]{:S(2)}) async-start(bf16[192,4,1024]{2,0,1:T(8,128)(2,1)} %bitcast.34), calls=%async_computation.2 | async-start | bytes 3145728 | tf_op jit(solution)/shard_map/all_to_all | solution.py:46
  85.2 0.0 copy-start.3
  85.2 0.0 copy-done.2
  85.2 1.3 copy.20
  86.5 0.0 copy-done.3
  86.6 11.7 %fusion.7 = f32[192,4096]{1,0:T(8,128)} fusion(bf16[192,1792]{1,0:T(8,128)(2,1)S(1)} %copy-done.3, bf16[4096,1792]{1,0:T(8,128)(2,1)} %param.7), kind=kOutput, calls=%fused_computation.17 | convolution fusion | flops 2818572288 | bytes 18513920 | tf_op jit(solution)/shard_map/dot_general | solution.py:8
  98.3 14.1 %all-to-all-done.1 = bf16[192,4,1024]{2,0,1:T(8,128)(2,1)S(1)} async-done(((bf16[192,4,1024]{2,0,1:T(8,128)(2,1)}), bf16[192,4,1024]{2,0,1:T(8,128)(2,1)S(1)}, u32[]{:S(2)}, u32[]{:S(2)}) %all-to-all-start.1) | async-done | bytes 1572896 | tf_op jit(solution)/shard_map/all_to_all | solution.py:46
  112.4 3.6 %all-to-all-start = ((bf16[192,4,1024]{2,0,1:T(8,128)(2,1)}), bf16[192,4,1024]{2,0,1:T(8,128)(2,1)S(1)}, u32[]{:S(2)}, u32[]{:S(2)}) async-start(bf16[192,4,1024]{2,0,1:T(8,128)(2,1)} %bitcast.36), calls=%async_computation.1 | async-start | bytes 3145728 | tf_op jit(solution)/shard_map/all_to_all | solution.py:45
  116.0 0.2 reduce-scatter.2.cloned.1.call-start
  116.2 12.3 %fusion = bf16[192,4096]{1,0:T(8,128)(2,1)} fusion(f32[192,4096]{1,0:T(8,128)} %fusion.7, bf16[192,1792]{1,0:T(8,128)(2,1)} %get-tuple-element.10, bf16[4096,1792]{1,0:T(8,128)(2,1)} %param.8), kind=kOutput, calls=%fused_computation.4 | convolution fusion | flops 2820145152 | bytes 20086784 | tf_op jit(solution)/shard_map/dot_general | solution.py:8
  128.5 0.0 reduce-scatter.2.cloned.1.call-update
  128.5 21.5 %all-gather.14.cloned.1.call-done = bf16[768,1792]{1,0:T(8,128)(2,1)} async-done(((bf16[192,1792]{1,0:T(8,128)(2,1)}), bf16[768,1792]{1,0:T(8,128)(2,1)}) %all-gather.14.cloned.1.call-update) | async-done | bytes 2752528 | tf_op jit(solution)/shard_map/all_gather | solution.py:49
  150.1 9.4 %convolution_convert_fusion = bf16[4,1792,1024]{2,1,0:T(8,128)(2,1)} fusion(bf16[4,192,1792]{2,1,0:T(8,128)(2,1)} %bitcast.39, bf16[192,4,1024]{2,0,1:T(8,128)(2,1)S(1)} %all-to-all-done.1), kind=kOutput, calls=%fused_computation.2 | convolution fusion | flops 2825912320 | bytes 19005440 | tf_op jit(solution)/shard_map/gth,gtd->ghd/dot_general | solution.py:65
  159.5 0.0 all-to-all-done
  159.5 31.0 %all-gather.12.cloned.1.call-done = bf16[768,1792]{1,0:T(8,128)(2,1)} async-done(((bf16[192,1792]{1,0:T(8,128)(2,1)}), bf16[768,1792]{1,0:T(8,128)(2,1)}) %all-gather.12.cloned.1.call-update) | async-done | bytes 2752528 | tf_op jit(solution)/shard_map/all_gather | solution.py:51
  190.5 9.5 %convert_bitcast_fusion = bf16[4,1024,1792]{1,2,0:T(8,128)(2,1)} fusion(bf16[4,192,1792]{2,1,0:T(8,128)(2,1)} %bitcast.38, bf16[192,4,1024]{2,0,1:T(8,128)(2,1)S(1)} %all-to-all-done), kind=kOutput, calls=%fused_computation | convolution fusion | flops 2825912320 | bytes 19005440 | tf_op jit(solution)/shard_map/gtd,gth->gdh/dot_general | solution.py:62
  200.0 11.1 %reduce_sum.38 = bf16[1792,1024]{1,0:T(8,128)(2,1)} reduce(bf16[4,1792,1024]{2,1,0:T(8,128)(2,1)} %convolution_convert_fusion, bf16[]{:T(256)} %constant.6.clone.1), dimensions={0}, to_apply=%region_3.0 | reduce | flops 5505024 | bytes 18350082 | tf_op jit(solution)/shard_map/reduce_sum | solution.py:16
  211.1 11.1 %reduce_sum.37 = bf16[1024,1792]{0,1:T(8,128)(2,1)} reduce(bf16[4,1024,1792]{1,2,0:T(8,128)(2,1)} %convert_bitcast_fusion, bf16[]{:T(256)} %constant.6.clone.1), dimensions={0}, to_apply=%region_2.0 | reduce | flops 5505024 | bytes 18350082 | tf_op jit(solution)/shard_map/reduce_sum | solution.py:16
  222.1 5.9 %copy.14 = bf16[1024,1792]{1,0:T(8,128)(2,1)} copy(bf16[1024,1792]{0,1:T(8,128)(2,1)} %reduce_sum.37) | data formatting | bytes 7340032
  228.1 4.8 %all-gather.10.cloned.1.call-done = bf16[768,1792]{1,0:T(8,128)(2,1)} async-done(((bf16[192,1792]{1,0:T(8,128)(2,1)}), bf16[768,1792]{1,0:T(8,128)(2,1)}) %all-gather.10.cloned.1.call-update) | async-done | bytes 2752528 | tf_op jit(solution)/shard_map/all_gather | solution.py:50
  232.8 9.4 %convert_bitcast_fusion.1 = bf16[4,1024,1792]{1,2,0:T(8,128)(2,1)} fusion(bf16[4,192,1792]{2,1,0:T(8,128)(2,1)} %bitcast.37, bf16[192,4,1024]{2,0,1:T(8,128)(2,1)S(1)} %all-to-all-done), kind=kOutput, calls=%fused_computation.1 | convolution fusion | flops 2825912320 | bytes 19005440 | tf_op jit(solution)/shard_map/gtd,gth->gdh/dot_general | solution.py:59
  242.2 11.0 %reduce_sum.36 = bf16[1024,1792]{0,1:T(8,128)(2,1)} reduce(bf16[4,1024,1792]{1,2,0:T(8,128)(2,1)} %convert_bitcast_fusion.1, bf16[]{:T(256)} %constant.6.clone.1), dimensions={0}, to_apply=%region_1.0 | reduce | flops 5505024 | bytes 18350082 | tf_op jit(solution)/shard_map/reduce_sum | solution.py:16
  253.2 5.9 %copy.13 = bf16[1024,1792]{1,0:T(8,128)(2,1)} copy(bf16[1024,1792]{0,1:T(8,128)(2,1)} %reduce_sum.36) | data formatting | bytes 7340032
  259.1 10.6 %reduce-scatter.2.cloned.1.call-done = bf16[24,4096]{1,0:T(8,128)(2,1)} async-done(((bf16[192,4096]{1,0:T(8,128)(2,1)}), bf16[24,4096]{1,0:T(8,128)(2,1)}) %reduce-scatter.2.cloned.1.call-update) | async-done | bytes 196624 | tf_op jit(solution)/shard_map/reduce_scatter | solution.py:34
Async XLA Ops:
  7.2 30.5 %all-gather.6.cloned.1.call-start = ((), (), s32[]{:S(2)}) async-start(), calls=%async_computation.3 | async-start | bytes 1769472 | tf_op jit(solution)/shard_map/all_gather | solution.py:22
  7.9 55.8 %all-gather.8.cloned.1.call-start = ((), (), s32[]{:S(2)}) async-start(), calls=%async_computation.4 | async-start | bytes 1769472 | tf_op jit(solution)/shard_map/all_gather | solution.py:21
  8.6 141.4 %all-gather.14.cloned.1.call-start = ((), (), s32[]{:S(2)}) async-start(), calls=%async_computation.8 | async-start | bytes 3440640 | tf_op jit(solution)/shard_map/all_gather | solution.py:49
  63.7 9.3 %copy-start.1 = (bf16[192,4096]{1,0:T(8,128)(2,1)S(1)}, bf16[192,4096]{1,0:T(8,128)(2,1)}, u32[]{:S(2)}) copy-start(bf16[192,4096]{1,0:T(8,128)(2,1)} %all-gather.8.cloned.1.call-done) | copy-start | bytes 4718596
  63.7 10.3 %copy-start.4 = (bf16[4096,1792]{1,0:T(8,128)(2,1)S(1)}, bf16[4096,1792]{1,0:T(8,128)(2,1)}, u32[]{:S(2)}) copy-start(bf16[4096,1792]{1,0:T(8,128)(2,1)} %param.8) | copy-start | bytes 44040196
  78.7 1.4 copy-start
  78.8 111.8 %all-gather.12.cloned.1.call-start = ((), (), s32[]{:S(2)}) async-start(), calls=%async_computation.7 | async-start | bytes 3440640 | tf_op jit(solution)/shard_map/all_gather | solution.py:51
  79.4 153.5 %all-gather.10.cloned.1.call-start = ((), (), s32[]{:S(2)}) async-start(), calls=%async_computation.6 | async-start | bytes 3440640 | tf_op jit(solution)/shard_map/all_gather | solution.py:50
  81.5 3.8 %copy-start.2 = (bf16[192,4096]{1,0:T(8,128)(2,1)S(1)}, bf16[192,4096]{1,0:T(8,128)(2,1)}, u32[]{:S(2)}) copy-start(bf16[192,4096]{1,0:T(8,128)(2,1)} %all-gather.8.cloned.1.call-done) | copy-start | bytes 4718596
  81.5 30.9 %all-to-all-start.1 = ((bf16[192,4,1024]{2,0,1:T(8,128)(2,1)}), bf16[192,4,1024]{2,0,1:T(8,128)(2,1)S(1)}, u32[]{:S(2)}, u32[]{:S(2)}) async-start(bf16[192,4,1024]{2,0,1:T(8,128)(2,1)} %bitcast.34), calls=%async_computation.2 | async-start | bytes 3145728 | tf_op jit(solution)/shard_map/all_to_all | solution.py:46
  85.2 1.3 copy-start.3
  112.4 47.1 %all-to-all-start = ((bf16[192,4,1024]{2,0,1:T(8,128)(2,1)}), bf16[192,4,1024]{2,0,1:T(8,128)(2,1)S(1)}, u32[]{:S(2)}, u32[]{:S(2)}) async-start(bf16[192,4,1024]{2,0,1:T(8,128)(2,1)} %bitcast.36), calls=%async_computation.1 | async-start | bytes 3145728 | tf_op jit(solution)/shard_map/all_to_all | solution.py:45
  116.0 153.8 %reduce-scatter.2.cloned.1.call-start = ((), (), s32[]{:S(2)}) async-start(), calls=%async_computation.5 | async-start | bytes 1769472 | tf_op jit(solution)/shard_map/reduce_scatter | solution.py:34
Sparse Core Ops, SparseCore 0:
  9.6 27.9 all-gather.5
  39.3 24.3 all-gather.7
  78.9 71.1 all-gather.13
  151.7 38.7 all-gather.11
  192.2 40.5 all-gather.9
  235.6 34.0 reduce-scatter.1
where the time goes:
time: 277 us
  waiting for transfers between devices  131 us (47%)
  matrix products  75 us (27%)
  other arithmetic  33.1 us (12%)
  local copies, waits for them, and re-layouts  15.7 us (6%)
  between operations  14.2 us (5%)
  starting transfers between devices  7.77 us (3%)
    reduce_sum x3, other arithmetic, group_total(): return jnp.sum(rounded.astype(jnp.float32), axis=0)  33.1 us
    dot_general x3, matrix products, contract_last(): lax.dot_general(left, right, (((1,), (1,)), ((), ())), preferred_element_...  32.7 us
    all_gather x1, waiting for transfers between devices, per_device(): lax.all_gather(grad_up_pre, 'dp', axis=0, tiled=True)  31 us
    all_gather x1, waiting for transfers between devices, per_device(): lax.all_gather(out_grad, 'tensor', axis=0, tiled=True)  28.9 us
    all_gather x1, waiting for transfers between devices, per_device(): lax.all_gather(hidden, 'dp', axis=0, tiled=True)  21.5 us
    all_gather x1, waiting for transfers between devices, per_device(): lax.all_gather(tokens, 'tensor', axis=0, tiled=True)  17.4 us
    all_to_all x1, waiting for transfers between devices, per_device(): lax.all_to_all(group_grads, 'dp', split_axis=1, concat_axis=0, tiled=True)  14.1 us
    unnamed x12, local copies, waits for them, and re-layouts  13.1 us
  transfers between devices with their start and end apart: 8, of which 7 were waited for; matrix products, arithmetic and copies ran while one was open for 39% of the time, Pallas kernels for 0%

commit v1 on v0

--- a/solution.py
+++ b/solution.py
@@ -19,7 +19,9 @@
 def per_device(tokens, out_grad, w_gate, w_up, w_down):
     group_tokens, group_grads = (
         lax.all_gather(tokens, "tensor", axis=0, tiled=True),
-        lax.all_gather(out_grad, "tensor", axis=0, tiled=True),
+        jnp.concatenate(
+            lax.all_to_all(jnp.stack([out_grad] * lax.axis_size("tensor")), "tensor", 0, 0), axis=0
+        ),
     )
     gate_val = jnp.dot(group_tokens, w_gate, preferred_element_type=jnp.float32)
     up_val = jnp.dot(group_tokens, w_up, preferred_element_type=jnp.float32)

time: 277 us -> 291 us (1.051)
  starting transfers between devices: 7.77 us -> 14 us
    all_to_all x0 -> x1, waiting for transfers between devices: none -> 49.7 us  [per_device(): lax.all_to_all(jnp.stack([out_grad] * lax.axis_size('tensor')), 'tensor',...]
    all_gather x1 -> x0, waiting for transfers between devices: 28.9 us -> none  [per_device(): lax.all_gather(out_grad, 'tensor', axis=0, tiled=True)]
    all_gather x1, waiting for transfers between devices: 17.4 us -> 0.02 us  [per_device(): lax.all_gather(tokens, 'tensor', axis=0, tiled=True)]
    all_to_all x0 -> x1, starting transfers between devices: none -> 6.35 us  [per_device(): lax.all_to_all(jnp.stack([out_grad] * lax.axis_size('tensor')), 'tensor',...]
    dot_general x1, matrix products: 4.76 us -> 9.83 us  [per_device(): up_val = jnp.dot(group_tokens, w_up, preferred_element_type=jnp.float32)]
    unnamed x12 -> x8, local copies, waits for them, and re-layouts: 13.1 us -> 11.9 us
  transfers between devices with their start and end apart: 8 -> 8, of which waited for: 7 -> 6; matrix products, arithmetic and copies ran while one was open for 39% -> 37% of each run, Pallas kernels for 0% -> 0%
where the time goes in v1:
time: 291 us; the launch traced here: 290 us
  waiting for transfers between devices  133 us (46%)
  matrix products  77.9 us (27%)
  other arithmetic  33.1 us (11%)
  local copies, waits for them, and re-layouts  18.2 us (6%)
  starting transfers between devices  14 us (5%)
  between operations  13.8 us (5%)
    all_to_all x1, waiting for transfers between devices, per_device(): lax.all_to_all(jnp.stack([out_grad] * lax.axis_size('tensor')), 'tensor',...  49.7 us
    reduce_sum x3, other arithmetic, group_total(): return jnp.sum(rounded.astype(jnp.float32), axis=0)  33.1 us
    all_gather x1, waiting for transfers between devices, per_device(): lax.all_gather(grad_up_pre, 'dp', axis=0, tiled=True)  32.6 us
    dot_general x3, matrix products, contract_last(): lax.dot_general(left, right, (((1,), (1,)), ((), ())), preferred_element_...  32.2 us
    all_gather x1, waiting for transfers between devices, per_device(): lax.all_gather(hidden, 'dp', axis=0, tiled=True)  20.7 us
    all_to_all x1, waiting for transfers between devices, per_device(): lax.all_to_all(group_grads, 'dp', split_axis=1, concat_axis=0, tiled=True)  13.1 us
    unnamed x8, local copies, waits for them, and re-layouts  11.9 us
    reduce_scatter x1, waiting for transfers between devices, per_device(): lax.psum_scatter((contract_last(grad_gate_pre, w_gate) + contract_last(gr...  10.6 us
  transfers between devices with their start and end apart: 8, of which 6 were waited for; matrix products, arithmetic and copies ran while one was open for 37% of the time, Pallas kernels for 0%

profile of v1, /device:TPU:0, one launch (start us, length us, event | category | flops | bytes accessed | tf_op | source)
XLA Modules:
  0.0 290.4 jit_solution(7800280475119002562)
XLA Ops:
  7.2 2.2 stack.2
  9.4 6.4 %all-to-all-start = ((bf16[8,24,4096]{2,1,0:T(8,128)(2,1)}), bf16[8,24,4096]{2,1,0:T(8,128)(2,1)S(1)}, u32[]{:S(2)}, u32[]{:S(2)}) async-start(bf16[8,24,4096]{2,1,0:T(8,128)(2,1)} %stack.2), calls=%async_computation | async-start | bytes 3145728 | tf_op jit(solution)/shard_map/all_to_all | solution.py:23
  15.8 0.0 all-gather.5.cloned.1.call-start
  15.8 0.7 all-gather.5.cloned.1.call-update
  16.5 0.0 all-gather.11.cloned.1.call-start
  16.5 49.7 %all-to-all-done = bf16[8,24,4096]{2,1,0:T(8,128)(2,1)S(1)} async-done(((bf16[8,24,4096]{2,1,0:T(8,128)(2,1)}), bf16[8,24,4096]{2,1,0:T(8,128)(2,1)S(1)}, u32[]{:S(2)}, u32[]{:S(2)}) %all-to-all-start) | async-done | bytes 1572896 | tf_op jit(solution)/shard_map/all_to_all | solution.py:23
  66.2 8.2 %fusion.5 = f32[192,1792]{1,0:T(8,128)S(1)} fusion(bf16[192,4096]{1,0:T(8,128)(2,1)S(1)} %bitcast.33, bf16[1792,4096]{1,0:T(8,128)(2,1)} %param.9), kind=kOutput, calls=%fused_computation.14 | convolution fusion | flops 2818572288 | bytes 17629184 | tf_op jit(solution)/shard_map/dot_general | solution.py:8
  74.4 0.0 all-gather.5.cloned.1.call-done
  74.4 0.0 copy-start
  74.5 7.6 %fusion.6 = f32[192,1792]{1,0:T(8,128)S(1)} fusion(bf16[192,4096]{1,0:T(8,128)(2,1)} %all-gather.5.cloned.1.call-done, bf16[4096,1792]{1,0:T(8,128)(2,1)} %param.7), kind=kOutput, calls=%fused_computation.15 | convolution fusion | flops 2818572288 | bytes 17629184 | tf_op jit(solution)/shard_map/dot_general | solution.py:26
  82.0 0.0 copy-done
  82.1 9.8 %multiply_convert_fusion = (bf16[192,1792]{1,0:T(8,128)(2,1)}, bf16[192,1792]{1,0:T(8,128)(2,1)}, bf16[192,1792]{1,0:T(8,128)(2,1)}) fusion(f32[192,1792]{1,0:T(8,128)S(1)} %fusion.6, f32[192,1792]{1,0:T(8,128)S(1)} %fusion.5, bf16[192,4096]{1,0:T(8,128)(2,1)S(1)} %copy-done, bf16[4096,1792]{1,0:T(8,128)(2,1)} %param.8), kind=kOutput, calls=%fused_computation.9 | convolution fusion | flops 2823733248 | bytes 21069824 | tf_op jit(solution)/shard_map/dot_general | solution.py:27
  91.9 0.0 all-gather.11.cloned.1.call-update
  91.9 0.0 all-gather.9.cloned.1.call-start
  92.0 0.7 all-gather.9.cloned.1.call-update
  92.6 0.0 all-gather.7.cloned.1.call-start
  92.7 0.5 all-gather.7.cloned.1.call-update
  93.2 1.2 all_to_all.31
  94.4 0.0 copy-start.1
  94.4 1.6 copy.12
  96.0 3.7 %all-to-all-start.2 = ((bf16[192,4,1024]{2,0,1:T(8,128)(2,1)}), bf16[192,4,1024]{2,0,1:T(8,128)(2,1)S(1)}, u32[]{:S(2)}, u32[]{:S(2)}) async-start(bf16[192,4,1024]{2,0,1:T(8,128)(2,1)} %copy.12), calls=%async_computation.3 | async-start | bytes 3145728 | tf_op jit(solution)/shard_map/all_to_all | solution.py:48
  99.7 0.0 copy-start.2
  99.8 0.0 copy-done.1
  99.8 1.3 copy.17
  101.0 0.0 copy-done.2
  101.1 11.7 %fusion.7 = f32[192,4096]{1,0:T(8,128)} fusion(bf16[192,1792]{1,0:T(8,128)(2,1)S(1)} %copy-done.2, bf16[4096,1792]{1,0:T(8,128)(2,1)} %param.7), kind=kOutput, calls=%fused_computation.16 | convolution fusion | flops 2818572288 | bytes 18513920 | tf_op jit(solution)/shard_map/dot_general | solution.py:8
  112.8 13.1 %all-to-all-done.2 = bf16[192,4,1024]{2,0,1:T(8,128)(2,1)S(1)} async-done(((bf16[192,4,1024]{2,0,1:T(8,128)(2,1)}), bf16[192,4,1024]{2,0,1:T(8,128)(2,1)S(1)}, u32[]{:S(2)}, u32[]{:S(2)}) %all-to-all-start.2) | async-done | bytes 1572896 | tf_op jit(solution)/shard_map/all_to_all | solution.py:48
  125.8 3.6 %all-to-all-start.1 = ((bf16[192,4,1024]{2,0,1:T(8,128)(2,1)}), bf16[192,4,1024]{2,0,1:T(8,128)(2,1)S(1)}, u32[]{:S(2)}, u32[]{:S(2)}) async-start(bf16[192,4,1024]{2,0,1:T(8,128)(2,1)} %bitcast.34), calls=%async_computation.2 | async-start | bytes 3145728 | tf_op jit(solution)/shard_map/all_to_all | solution.py:47
  129.4 0.2 reduce-scatter.2.cloned.1.call-start
  129.6 12.3 %fusion = bf16[192,4096]{1,0:T(8,128)(2,1)} fusion(f32[192,4096]{1,0:T(8,128)} %fusion.7, bf16[192,1792]{1,0:T(8,128)(2,1)} %get-tuple-element.10, bf16[4096,1792]{1,0:T(8,128)(2,1)} %param.8), kind=kOutput, calls=%fused_computation.4 | convolution fusion | flops 2820145152 | bytes 20086784 | tf_op jit(solution)/shard_map/dot_general | solution.py:8
  141.9 0.0 reduce-scatter.2.cloned.1.call-update
  141.9 20.7 %all-gather.11.cloned.1.call-done = bf16[768,1792]{1,0:T(8,128)(2,1)} async-done(((bf16[192,1792]{1,0:T(8,128)(2,1)}), bf16[768,1792]{1,0:T(8,128)(2,1)}) %all-gather.11.cloned.1.call-update) | async-done | bytes 2752528 | tf_op jit(solution)/shard_map/all_gather | solution.py:51
  162.7 9.4 %convolution_convert_fusion = bf16[4,1792,1024]{2,1,0:T(8,128)(2,1)} fusion(bf16[4,192,1792]{2,1,0:T(8,128)(2,1)} %bitcast.37, bf16[192,4,1024]{2,0,1:T(8,128)(2,1)S(1)} %all-to-all-done.2), kind=kOutput, calls=%fused_computation.2 | convolution fusion | flops 2825912320 | bytes 19005440 | tf_op jit(solution)/shard_map/gth,gtd->ghd/dot_general | solution.py:67
  172.1 0.0 all-to-all-done.1
  172.1 32.6 %all-gather.9.cloned.1.call-done = bf16[768,1792]{1,0:T(8,128)(2,1)} async-done(((bf16[192,1792]{1,0:T(8,128)(2,1)}), bf16[768,1792]{1,0:T(8,128)(2,1)}) %all-gather.9.cloned.1.call-update) | async-done | bytes 2752528 | tf_op jit(solution)/shard_map/all_gather | solution.py:53
  204.7 9.5 %convert_bitcast_fusion = bf16[4,1024,1792]{1,2,0:T(8,128)(2,1)} fusion(bf16[4,192,1792]{2,1,0:T(8,128)(2,1)} %bitcast.36, bf16[192,4,1024]{2,0,1:T(8,128)(2,1)S(1)} %all-to-all-done.1), kind=kOutput, calls=%fused_computation | convolution fusion | flops 2825912320 | bytes 19005440 | tf_op jit(solution)/shard_map/gtd,gth->gdh/dot_general | solution.py:64
  214.2 11.1 %reduce_sum.38 = bf16[1792,1024]{1,0:T(8,128)(2,1)} reduce(bf16[4,1792,1024]{2,1,0:T(8,128)(2,1)} %convolution_convert_fusion, bf16[]{:T(256)} %constant.6.clone.1), dimensions={0}, to_apply=%region_3.0 | reduce | flops 5505024 | bytes 18350082 | tf_op jit(solution)/shard_map/reduce_sum | solution.py:16
  225.2 11.1 %reduce_sum.37 = bf16[1024,1792]{0,1:T(8,128)(2,1)} reduce(bf16[4,1024,1792]{1,2,0:T(8,128)(2,1)} %convert_bitcast_fusion, bf16[]{:T(256)} %constant.6.clone.1), dimensions={0}, to_apply=%region_2.0 | reduce | flops 5505024 | bytes 18350082 | tf_op jit(solution)/shard_map/reduce_sum | solution.py:16
  236.3 5.9 %copy.14 = bf16[1024,1792]{1,0:T(8,128)(2,1)} copy(bf16[1024,1792]{0,1:T(8,128)(2,1)} %reduce_sum.37) | data formatting | bytes 7340032
  242.2 4.8 %all-gather.7.cloned.1.call-done = bf16[768,1792]{1,0:T(8,128)(2,1)} async-done(((bf16[192,1792]{1,0:T(8,128)(2,1)}), bf16[768,1792]{1,0:T(8,128)(2,1)}) %all-gather.7.cloned.1.call-update) | async-done | bytes 2752528 | tf_op jit(solution)/shard_map/all_gather | solution.py:52
  247.0 9.4 %convert_bitcast_fusion.1 = bf16[4,1024,1792]{1,2,0:T(8,128)(2,1)} fusion(bf16[4,192,1792]{2,1,0:T(8,128)(2,1)} %bitcast.35, bf16[192,4,1024]{2,0,1:T(8,128)(2,1)S(1)} %all-to-all-done.1), kind=kOutput, calls=%fused_computation.1 | convolution fusion | flops 2825912320 | bytes 19005440 | tf_op jit(solution)/shard_map/gtd,gth->gdh/dot_general | solution.py:61
  256.3 11.0 %reduce_sum.36 = bf16[1024,1792]{0,1:T(8,128)(2,1)} reduce(bf16[4,1024,1792]{1,2,0:T(8,128)(2,1)} %convert_bitcast_fusion.1, bf16[]{:T(256)} %constant.6.clone.1), dimensions={0}, to_apply=%region_1.0 | reduce | flops 5505024 | bytes 18350082 | tf_op jit(solution)/shard_map/reduce_sum | solution.py:16
  267.3 5.9 %copy.13 = bf16[1024,1792]{1,0:T(8,128)(2,1)} copy(bf16[1024,1792]{0,1:T(8,128)(2,1)} %reduce_sum.36) | data formatting | bytes 7340032
  273.3 10.6 %reduce-scatter.2.cloned.1.call-done = bf16[24,4096]{1,0:T(8,128)(2,1)} async-done(((bf16[192,4096]{1,0:T(8,128)(2,1)}), bf16[24,4096]{1,0:T(8,128)(2,1)}) %reduce-scatter.2.cloned.1.call-update) | async-done | bytes 196624 | tf_op jit(solution)/shard_map/reduce_scatter | solution.py:36
Async XLA Ops:
  9.4 56.8 %all-to-all-start = ((bf16[8,24,4096]{2,1,0:T(8,128)(2,1)}), bf16[8,24,4096]{2,1,0:T(8,128)(2,1)S(1)}, u32[]{:S(2)}, u32[]{:S(2)}) async-start(bf16[8,24,4096]{2,1,0:T(8,128)(2,1)} %stack.2), calls=%async_computation | async-start | bytes 3145728 | tf_op jit(solution)/shard_map/all_to_all | solution.py:23
  15.8 58.7 %all-gather.5.cloned.1.call-start = ((), (), s32[]{:S(2)}) async-start(), calls=%async_computation.4 | async-start | bytes 1769472 | tf_op jit(solution)/shard_map/all_gather | solution.py:21
  16.5 146.2 %all-gather.11.cloned.1.call-start = ((), (), s32[]{:S(2)}) async-start(), calls=%async_computation.8 | async-start | bytes 3440640 | tf_op jit(solution)/shard_map/all_gather | solution.py:51
  74.4 7.6 %copy-start = (bf16[192,4096]{1,0:T(8,128)(2,1)S(1)}, bf16[192,4096]{1,0:T(8,128)(2,1)}, u32[]{:S(2)}) copy-start(bf16[192,4096]{1,0:T(8,128)(2,1)} %all-gather.5.cloned.1.call-done) | copy-start | bytes 4718596
  91.9 112.8 %all-gather.9.cloned.1.call-start = ((), (), s32[]{:S(2)}) async-start(), calls=%async_computation.7 | async-start | bytes 3440640 | tf_op jit(solution)/shard_map/all_gather | solution.py:53
  92.6 154.3 %all-gather.7.cloned.1.call-start = ((), (), s32[]{:S(2)}) async-start(), calls=%async_computation.6 | async-start | bytes 3440640 | tf_op jit(solution)/shard_map/all_gather | solution.py:52
  94.4 5.3 %copy-start.1 = (bf16[192,4096]{1,0:T(8,128)(2,1)S(1)}, bf16[192,4096]{1,0:T(8,128)(2,1)}, u32[]{:S(2)}) copy-start(bf16[192,4096]{1,0:T(8,128)(2,1)} %all-gather.5.cloned.1.call-done) | copy-start | bytes 4718596
  96.0 29.8 %all-to-all-start.2 = ((bf16[192,4,1024]{2,0,1:T(8,128)(2,1)}), bf16[192,4,1024]{2,0,1:T(8,128)(2,1)S(1)}, u32[]{:S(2)}, u32[]{:S(2)}) async-start(bf16[192,4,1024]{2,0,1:T(8,128)(2,1)} %copy.12), calls=%async_computation.3 | async-start | bytes 3145728 | tf_op jit(solution)/shard_map/all_to_all | solution.py:48
  99.7 1.3 copy-start.2
  125.8 46.3 %all-to-all-start.1 = ((bf16[192,4,1024]{2,0,1:T(8,128)(2,1)}), bf16[192,4,1024]{2,0,1:T(8,128)(2,1)S(1)}, u32[]{:S(2)}, u32[]{:S(2)}) async-start(bf16[192,4,1024]{2,0,1:T(8,128)(2,1)} %bitcast.34), calls=%async_computation.2 | async-start | bytes 3145728 | tf_op jit(solution)/shard_map/all_to_all | solution.py:47
  129.4 154.4 %reduce-scatter.2.cloned.1.call-start = ((), (), s32[]{:S(2)}) async-start(), calls=%async_computation.5 | async-start | bytes 1769472 | tf_op jit(solution)/shard_map/reduce_scatter | solution.py:36
Sparse Core Ops, SparseCore 0:
  18.2 44.5 all-gather.4
  92.0 70.5 all-gather.10
  164.5 40.1 all-gather.8
  206.4 40.5 all-gather.6
  249.7 34.0 reduce-scatter.1
